TPU v7x, 32 devices: a whole 2x2x4 slice. The times are simulated.
32 devices in a mesh: chan: 4 (over x, core), az: 8 (over z, y).
Axes of the slice: x: 2, y: 2, z: 4, core: 2. Of those that a mesh axis runs over, the one named last changes fastest.
Arguments:
- signal: bfloat16 [4, 2, 128, 8192], P('chan', None, 'az'), may hold values from -6 to 6
- tap_table: float32 [64, 16], replicated, may hold values from -1.5 to 1.5
- range_shift: int32 [1024], P('az'), may hold values from -8 to 8
- tap_index: int32 [1024], P('az'), may hold values from 0 to 63
- ref_channel: int32 [8], P('az'), may hold values from 0 to 3
Outputs:
- picture: float32 [4, 2, 128, 1024], P('chan', None, None, 'az')
All inputs are finite; a program needn't handle non-finite values.
Results may differ from a plain program's by a relative error of at most 0.012.
Values may be sent and summed in bfloat16 or wider, within the bound.
A program may use at most 64 MiB of HBM per device.

v0:
```python
import math
import jax
import jax.numpy as jnp
from jax import lax
from jax.sharding import PartitionSpec as P

RF1 = 64
RF2 = 128
TAPS = 16
NTAB = 64
GUARD = 16
HALO = 16
PRECISE = lax.Precision.HIGH


def dft_table(length, orient):
    counter = jnp.arange(length, dtype=jnp.int32)
    phase = counter[:, None] * counter[None, :] % length
    angle = 2.0 * math.pi / length * phase.astype(jnp.float32)
    return (jnp.cos(angle), orient * jnp.sin(angle))


def twiddle_table(lead_size, tail_size, orient):
    lead_idx = jnp.arange(lead_size, dtype=jnp.int32)
    tail_idx = jnp.arange(tail_size, dtype=jnp.int32)
    phase = lead_idx[:, None] * tail_idx[None, :] % (lead_size * tail_size)
    angle = 2.0 * math.pi / (lead_size * tail_size) * phase.astype(jnp.float32)
    return (jnp.cos(angle), orient * jnp.sin(angle))


def split_table(table):
    upper = table.astype(jnp.bfloat16)
    lower = (table - upper.astype(jnp.float32)).astype(jnp.bfloat16)
    return (upper, lower)


def lead_product(table, data):
    if data.dtype == jnp.bfloat16:
        upper, lower = split_table(table)
        first = jnp.einsum("ka,rab->rkb", upper, data, preferred_element_type=jnp.float32)
        return first + jnp.einsum("ka,rab->rkb", lower, data, preferred_element_type=jnp.float32)
    return jnp.einsum("ka,rab->rkb", table, data, precision=PRECISE)


def along_last(real_part, imag_part, lead_size, tail_size, orient, factor):
    height = real_part.shape[0]
    real_in = real_part.reshape(height, lead_size, tail_size)
    imag_in = imag_part.reshape(height, lead_size, tail_size)
    lead_cos, lead_sin = dft_table(lead_size, orient)
    step_real = lead_product(lead_cos, real_in) - lead_product(lead_sin, imag_in)
    step_imag = lead_product(lead_cos, imag_in) + lead_product(lead_sin, real_in)
    twist_cos, twist_sin = twiddle_table(lead_size, tail_size, orient)
    turned_real = step_real * twist_cos[None] - step_imag * twist_sin[None]
    turned_imag = step_real * twist_sin[None] + step_imag * twist_cos[None]
    tail_cos, tail_sin = dft_table(tail_size, orient)
    out_real = jnp.einsum("rkb,bm->rmk", turned_real, tail_cos, precision=PRECISE) - jnp.einsum(
        "rkb,bm->rmk", turned_imag, tail_sin, precision=PRECISE
    )
    out_imag = jnp.einsum("rkb,bm->rmk", turned_real, tail_sin, precision=PRECISE) + jnp.einsum(
        "rkb,bm->rmk", turned_imag, tail_cos, precision=PRECISE
    )
    return (factor * out_real.reshape(height, -1), factor * out_imag.reshape(height, -1))


def along_first(real_part, imag_part, lead_size, tail_size, orient, factor):
    columns = real_part.shape[1]
    real_in = real_part.reshape(lead_size, tail_size, columns)
    imag_in = imag_part.reshape(lead_size, tail_size, columns)
    lead_cos, lead_sin = dft_table(lead_size, orient)
    step_real = jnp.einsum("ka,abs->kbs", lead_cos, real_in, precision=PRECISE) - jnp.einsum(
        "ka,abs->kbs", lead_sin, imag_in, precision=PRECISE
    )
    step_imag = jnp.einsum("ka,abs->kbs", lead_cos, imag_in, precision=PRECISE) + jnp.einsum(
        "ka,abs->kbs", lead_sin, real_in, precision=PRECISE
    )
    twist_cos, twist_sin = twiddle_table(lead_size, tail_size, orient)
    turned_real = step_real * twist_cos[:, :, None] - step_imag * twist_sin[:, :, None]
    turned_imag = step_real * twist_sin[:, :, None] + step_imag * twist_cos[:, :, None]
    tail_cos, tail_sin = dft_table(tail_size, orient)
    out_real = jnp.einsum("kbs,bm->mks", turned_real, tail_cos, precision=PRECISE) - jnp.einsum(
        "kbs,bm->mks", turned_imag, tail_sin, precision=PRECISE
    )
    out_imag = jnp.einsum("kbs,bm->mks", turned_real, tail_sin, precision=PRECISE) + jnp.einsum(
        "kbs,bm->mks", turned_imag, tail_cos, precision=PRECISE
    )
    return (factor * out_real.reshape(-1, columns), factor * out_imag.reshape(-1, columns))


def whiten(spec_real, spec_imag):
    inverse = lax.rsqrt(jnp.maximum(spec_real * spec_real + spec_imag * spec_imag, 1.0))
    return ((spec_real * inverse).astype(jnp.bfloat16), (-spec_imag * inverse).astype(jnp.bfloat16))


def band_product(frame, band_upper, band_lower):
    first = jnp.dot(frame, band_upper, preferred_element_type=jnp.float32)
    return first + jnp.dot(frame, band_lower, preferred_element_type=jnp.float32)


def shards(signal, tap_table, range_shift, tap_index, ref_channel):
    source_id = ref_channel[0]
    is_source = lax.axis_index("chan") == source_id
    own_data = signal[0]
    pul_dev = own_data.shape[1]
    samples_len = own_data.shape[2]
    slab_len = range_shift.shape[0]
    az_count = lax.axis_size("az")
    lag_count = slab_len * az_count
    factor_range = 1.0 / math.sqrt(samples_len)
    spec_real, spec_imag = along_last(own_data[0], own_data[1], RF1, RF2, -1.0, factor_range)
    masked_data = jnp.where(is_source, own_data, jnp.zeros_like(own_data))
    ref_data = lax.psum(masked_data, "chan").astype(jnp.float32).astype(jnp.bfloat16)
    ref_real, ref_imag = along_last(ref_data[0], ref_data[1], RF1, RF2, -1.0, factor_range)
    filter_low_real, filter_low_imag = whiten(ref_real, ref_imag)
    filter_real = filter_low_real.astype(jnp.float32)
    filter_imag = filter_low_imag.astype(jnp.float32)
    prod_real = spec_real * filter_real - spec_imag * filter_imag
    prod_imag = spec_real * filter_imag + spec_imag * filter_real
    lag_real, lag_imag = along_last(prod_real, prod_imag, RF1, RF2, 1.0, factor_range)
    compressed = jnp.stack(
        [lag_real[:, GUARD : GUARD + lag_count], lag_imag[:, GUARD : GUARD + lag_count]]
    ).astype(jnp.bfloat16)
    padded = jnp.pad(compressed, ((0, 0), (0, 0), (HALO, slab_len + HALO)))
    main_part = padded[:, :, :lag_count].reshape(2, pul_dev, az_count, slab_len)
    after_part = padded[:, :, slab_len : slab_len + lag_count].reshape(
        2, pul_dev, az_count, slab_len
    )[..., : 2 * HALO]
    widened = jnp.concatenate([main_part, after_part], axis=3).reshape(
        2, pul_dev, az_count * (slab_len + 2 * HALO)
    )
    framed = lax.all_to_all(widened, "az", split_axis=2, concat_axis=1, tiled=True)
    chooser = (tap_index[:, None] == jnp.arange(NTAB, dtype=jnp.int32)[None, :]).astype(jnp.float32)
    tap_rows = jnp.dot(chooser, tap_table, precision=lax.Precision.HIGHEST)
    source_pos = jnp.arange(slab_len + 2 * HALO, dtype=jnp.int32)[:, None, None]
    target_pos = (
        jnp.arange(slab_len, dtype=jnp.int32)[None, :, None]
        + HALO
        + range_shift[None, :, None]
        + jnp.arange(TAPS, dtype=jnp.int32)[None, None, :]
        - TAPS // 2
    )
    banded = jnp.sum(jnp.where(source_pos == target_pos, tap_rows[None], 0.0), axis=2)
    band_upper, band_lower = split_table(banded)
    aligned_real = band_product(framed[0], band_upper, band_lower)
    aligned_imag = band_product(framed[1], band_upper, band_lower)
    pulse_total = aligned_real.shape[0]
    doppler_real, doppler_imag = along_first(
        aligned_real, aligned_imag, az_count, pul_dev, -1.0, 1.0 / math.sqrt(pulse_total)
    )
    return jnp.stack([doppler_real, doppler_imag])[None]


def solution(mesh):
    return jax.shard_map(
        shards,
        mesh=mesh,
        in_specs=(P("chan", None, "az", None), P(), P("az"), P("az"), P("az")),
        out_specs=P("chan", None, None, "az"),
        check_vma=False,
    )
```

profile of v0, /device:TPU:0, one launch (start us, length us, event | category | flops | bytes accessed | tf_op | source)
XLA Modules:
  0.0 95.3 jit_solution(10513515113329657731)
XLA Ops:
  7.3 0.8 select_bitcast_fusion
  11.7 0.6 fusion.27
  12.4 0.6 fusion.10
  13.1 0.6 fusion.5
  15.6 30.3 %all-reduce.3.cloned.1.call-done = bf16[2,16,8192]{2,1,0:T(8,128)(2,1)} async-done(((bf16[2,16,8192]{2,1,0:T(8,128)(2,1)}), bf16[2,16,8192]{2,1,0:T(8,128)(2,1)}) %all-reduce.3.cloned.1.call-update) | async-done | bytes 524304 | tf_op jit(solution)/shard_map/psum | solution.py:111
  45.9 1.1 %slice_bitcast_fusion = (bf16[2,8,64,128]{3,1,2,0:T(8,128)(2,1)S(1)}, bf16[2,8,64,128]{3,1,2,0:T(8,128)(2,1)S(1)}) fusion(bf16[2,16,8192]{2,1,0:T(8,128)(2,1)} %all-reduce.3.cloned.1.call-done), kind=kLoop, calls=%fused_computation.71 | loop fusion | bytes 1048576
  50.3 1.4 %fusion.33 = f32[128,16,64]{0,2,1:T(8,128)} fusion(f32[16,64,128]{2,1,0:T(8,128)S(1)} %fusion.16, f32[16,64,128]{2,1,0:T(8,128)S(1)} %fusion.14, f32[64,128]{1,0:T(8,128)S(1)} %get-tuple-element.19, f32[64,128]{1,0:T(8,128)S(1)} %get-tuple-element.20), kind=kOutput, calls=%fused_computation.79 | convolution fusion | flops 101285888 | bytes 1638400 | tf_op jit(solution)/shard_map/rkb,bm->rmk/dot_general | solution.py:56
  51.7 1.6 %negate_bitcast_fusion = (f32[16,128,64]{1,2,0:T(8,128)}, f32[16,128,64]{1,2,0:T(8,128)}) fusion(f32[128,16,64]{0,2,1:T(8,128)S(1)} %fusion.32, f32[16,64,128]{2,1,0:T(8,128)S(1)} %fusion.16, f32[16,64,128]{2,1,0:T(8,128)S(1)} %fusion.14, f32[64,128]{1,0:T(8,128)S(1)} %get-tuple-element.19, f32[64,128]{1,0:T(8,128)S(1)} %get-tuple-element.20), kind=kOutput, calls=%fused_computation.62 | convolution fusion | flops 101810176 | bytes 2686976 | tf_op jit(solution)/shard_map/rkb,bm->rmk/dot_general | solution.py:59
  53.3 1.4 %copy.77 = f32[16,128,64]{2,1,0:T(8,128)S(1)} copy(f32[16,128,64]{1,2,0:T(8,128)} %get-tuple-element.8) | data formatting | bytes 1048576 | tf_op jit(solution)/shard_map/mul | solution.py:90
  54.7 1.0 %mul.962 = f32[16,64,128]{2,1,0:T(8,128)} reshape(f32[16,128,64]{2,1,0:T(8,128)S(1)} %copy.77) | data formatting | bytes 1048576 | tf_op jit(solution)/shard_map/mul | solution.py:90
  55.7 1.4 %copy.79 = f32[16,128,64]{2,1,0:T(8,128)S(1)} copy(f32[16,128,64]{1,2,0:T(8,128)} %get-tuple-element.7) | data formatting | bytes 1048576 | tf_op jit(solution)/shard_map/neg | solution.py:91
  57.1 1.0 %neg.13 = f32[16,64,128]{2,1,0:T(8,128)} reshape(f32[16,128,64]{2,1,0:T(8,128)S(1)} %copy.79) | data formatting | bytes 1048576 | tf_op jit(solution)/shard_map/neg | solution.py:91
  58.1 1.7 %fusion.8 = f32[16,128,64]{1,2,0:T(8,128)S(1)} fusion(f32[128,16,64]{0,2,1:T(8,128)} %fusion.33, f32[16,64,128]{2,1,0:T(8,128)S(1)} %fusion.16, f32[16,64,128]{2,1,0:T(8,128)S(1)} %fusion.14, f32[64,128]{1,0:T(8,128)S(1)} %get-tuple-element.19, f32[64,128]{1,0:T(8,128)S(1)} %get-tuple-element.20), kind=kOutput, calls=%fused_computation.25 | convolution fusion | flops 101564416 | bytes 2162688 | tf_op jit(solution)/shard_map/rkb,bm->rmk/dot_general | solution.py:56
  60.1 1.0 %mul.957 = f32[16,64,128]{2,1,0:T(8,128)} reshape(f32[16,128,64]{2,1,0:T(8,128)S(1)} %copy.76) | data formatting | bytes 1048576 | tf_op jit(solution)/shard_map/mul | solution.py:62
  61.5 1.2 %multiply_convert_fusion = (bf16[16,64,128]{2,1,0:T(8,128)(2,1)S(1)}, bf16[16,64,128]{2,1,0:T(8,128)(2,1)S(1)}) fusion(f32[16,64,128]{2,1,0:T(8,128)S(1)} %copy-done.3, f32[16,64,128]{2,1,0:T(8,128)S(1)} %copy-done.2, f32[16,64,128]{2,1,0:T(8,128)} %mul.957), kind=kLoop, calls=%fused_computation.61 | loop fusion | flops 917504 | bytes 2097152 | tf_op jit(solution)/shard_map/convert_element_type | solution.py:91
  62.7 0.7 fusion.84
  66.4 0.6 fusion.20
  67.9 0.6 fusion.19
  69.5 0.7 copy.82
  70.3 1.3 %reshape.214 = bf16[8,2,2560]{2,1,0:T(2,128)(2,1)} reshape(bf16[1280,2,16]{2,1,0:T(2,128)(2,1)S(1)} %bitcast.209) | data formatting | bytes 163840
  71.6 5.5 %all-to-all-start = ((bf16[8,2,2560]{2,1,0:T(2,128)(2,1)}), bf16[8,2,2560]{2,1,0:T(2,128)(2,1)S(1)}, u32[]{:S(2)}, u32[]{:S(2)}) async-start(bf16[8,2,2560]{2,1,0:T(2,128)(2,1)} %reshape.214), calls=%async_computation | async-start | bytes 163840 | tf_op jit(solution)/shard_map/all_to_all | solution.py:130
  77.5 6.7 %all-to-all-done = bf16[8,2,2560]{2,1,0:T(2,128)(2,1)S(1)} async-done(((bf16[8,2,2560]{2,1,0:T(2,128)(2,1)}), bf16[8,2,2560]{2,1,0:T(2,128)(2,1)S(1)}, u32[]{:S(2)}, u32[]{:S(2)}) %all-to-all-start) | async-done | bytes 81952 | tf_op jit(solution)/shard_map/all_to_all | solution.py:130
  84.6 0.6 copy.96
  87.8 0.7 maximum_bitcast_fusion
  (83 shorter events, 17.3 us)
Async XLA Ops:
  6.5 8.4 %copy-start = (f32[64,16]{0,1:T(8,128)S(1)}, f32[64,16]{0,1:T(8,128)}, u32[]{:S(2)}) copy-start(f32[64,16]{0,1:T(8,128)} %param.6) | copy-start | bytes 12292
  6.5 1.7 %copy-start.1 = (bf16[1,2,16,8192]{3,2,1,0:T(8,128)(2,1)S(1)}, bf16[1,2,16,8192]{3,2,1,0:T(8,128)(2,1)}, u32[]{:S(2)}) copy-start(bf16[1,2,16,8192]{3,2,1,0:T(8,128)(2,1)} %param.5) | copy-start | bytes 1572868
  6.5 39.3 %all-reduce.3.cloned.1.call-start = ((), (), s32[]{:S(2)}) async-start(), calls=%async_computation.1 | async-start | bytes 1048576 | tf_op jit(solution)/shard_map/psum | solution.py:111
  13.1 0.7 copy-start.4
  14.7 0.7 copy-start.5
  60.1 1.0 %copy-start.2 = (f32[16,64,128]{2,1,0:T(8,128)S(1)}, f32[16,64,128]{2,1,0:T(8,128)}, u32[]{:S(2)}) copy-start(f32[16,64,128]{2,1,0:T(8,128)} %mul.962) | copy-start | bytes 1572868
  60.1 1.4 %copy-start.3 = (f32[16,64,128]{2,1,0:T(8,128)S(1)}, f32[16,64,128]{2,1,0:T(8,128)}, u32[]{:S(2)}) copy-start(f32[16,64,128]{2,1,0:T(8,128)} %neg.13) | copy-start | bytes 1572868
  71.6 12.5 %all-to-all-start = ((bf16[8,2,2560]{2,1,0:T(2,128)(2,1)}), bf16[8,2,2560]{2,1,0:T(2,128)(2,1)S(1)}, u32[]{:S(2)}, u32[]{:S(2)}) async-start(bf16[8,2,2560]{2,1,0:T(2,128)(2,1)} %reshape.214), calls=%async_computation | async-start | bytes 163840 | tf_op jit(solution)/shard_map/all_to_all | solution.py:130
Sparse Core Ops, SparseCore 0:
  9.7 36.1 all-reduce.2
where the time goes:
time: 95.7 us; the launch traced here: 95.3 us
  waiting for transfers between devices  37 us (39%)
  matrix products  20.2 us (21%)
  between operations  14.7 us (15%)
  local copies, waits for them, and re-layouts  14.3 us (15%)
  starting transfers between devices  5.52 us (6%)
  other arithmetic  3.55 us (4%)
    psum x1, waiting for transfers between devices, shards(): lax.psum(masked_data, 'chan').astype(jnp.float32).astype(jnp.bfloat16)  30.3 us
    all_to_all x1, waiting for transfers between devices, shards(): lax.all_to_all(widened, 'az', split_axis=2, concat_axis=1, tiled=True)  6.7 us
    all_to_all x1, starting transfers between devices, shards(): lax.all_to_all(widened, 'az', split_axis=2, concat_axis=1, tiled=True)  5.52 us
    unnamed x22, local copies, waits for them, and re-layouts  3.93 us
    dot_general x3, matrix products, along_last(): jnp.einsum('rkb,bm->rmk', turned_imag, tail_sin, precision=PRECISE)  2.91 us
    dot_general x3, matrix products, along_last(): jnp.einsum('rkb,bm->rmk', turned_imag, tail_cos, precision=PRECISE)  2.87 us
    mul x6, local copies, waits for them, and re-layouts, along_last(): factor * out_real.reshape(height, -1)  2.63 us
    dot_general x3, matrix products, along_last(): jnp.einsum('rkb,bm->rmk', turned_real, tail_cos, precision=PRECISE)  2.63 us
  transfers between devices with their start and end apart: 2, of which 2 were waited for; matrix products, arithmetic and copies ran while one was open for 7% of the time, Pallas kernels for 0%

commit v1 on v0

--- a/solution.py
+++ b/solution.py
@@ -108,7 +108,11 @@
     factor_range = 1.0 / math.sqrt(samples_len)
     spec_real, spec_imag = along_last(own_data[0], own_data[1], RF1, RF2, -1.0, factor_range)
     masked_data = jnp.where(is_source, own_data, jnp.zeros_like(own_data))
-    ref_data = lax.psum(masked_data, "chan").astype(jnp.float32).astype(jnp.bfloat16)
+    ref_data = (
+        jnp.sum(lax.all_gather(masked_data, "chan"), axis=0)
+        .astype(jnp.float32)
+        .astype(jnp.bfloat16)
+    )
     ref_real, ref_imag = along_last(ref_data[0], ref_data[1], RF1, RF2, -1.0, factor_range)
     filter_low_real, filter_low_imag = whiten(ref_real, ref_imag)
     filter_real = filter_low_real.astype(jnp.float32)

time: 95.7 us -> 86.5 us (0.904)
  waiting for transfers between devices: 37 us -> 25.7 us
  other arithmetic: 3.55 us -> 5.7 us
    psum x1 -> x0, waiting for transfers between devices: 30.3 us -> none  [shards(): lax.psum(masked_data, 'chan').astype(jnp.float32).astype(jnp.bfloat16)]
    all_gather x0 -> x1, waiting for transfers between devices: none -> 19 us  [shards(): lax.all_gather(masked_data, 'chan')]
    reduce_sum x0 -> x1, other arithmetic: none -> 1.98 us  [shards(): jnp.sum(lax.all_gather(masked_data, 'chan'), axis=0).astype(jnp.float32)]
    unnamed x22, local copies, waits for them, and re-layouts: 3.93 us -> 2.1 us
    mul x6, local copies, waits for them, and re-layouts: 2.63 us -> 3.78 us  [along_last(): factor * out_real.reshape(height, -1)]
  transfers between devices with their start and end apart: 2 -> 2, of which waited for: 2 -> 2; matrix products, arithmetic and copies ran while one was open for 7% -> 8% of each run, Pallas kernels for 0% -> 0%
where the time goes in v1:
time: 86.5 us; the launch traced here: 86.1 us
  waiting for transfers between devices  25.7 us (30%)
  matrix products  20.9 us (24%)
  between operations  14.7 us (17%)
  local copies, waits for them, and re-layouts  13.6 us (16%)
  other arithmetic  5.7 us (7%)
  starting transfers between devices  5.51 us (6%)
    all_gather x1, waiting for transfers between devices, shards(): lax.all_gather(masked_data, 'chan')  19 us
    all_to_all x1, waiting for transfers between devices, shards(): lax.all_to_all(widened, 'az', split_axis=2, concat_axis=1, tiled=True)  6.7 us
    all_to_all x1, starting transfers between devices, shards(): lax.all_to_all(widened, 'az', split_axis=2, concat_axis=1, tiled=True)  5.51 us
    mul x6, local copies, waits for them, and re-layouts, along_last(): factor * out_real.reshape(height, -1)  3.78 us
    dot_general x3, matrix products, along_last(): jnp.einsum('rkb,bm->rmk', turned_imag, tail_sin, precision=PRECISE)  3.71 us
    dot_general x3, matrix products, along_last(): jnp.einsum('rkb,bm->rmk', turned_imag, tail_cos, precision=PRECISE)  2.83 us
    dot_general x3, matrix products, along_last(): jnp.einsum('rkb,bm->rmk', turned_real, tail_cos, precision=PRECISE)  2.64 us
    dot_general x8, matrix products, lead_product(): jnp.einsum('ka,rab->rkb', lower, data, preferred_element_type=jnp.float32)  2.6 us
  transfers between devices with their start and end apart: 2, of which 2 were waited for; matrix products, arithmetic and copies ran while one was open for 8% of the time, Pallas kernels for 0%

profile of v1, /device:TPU:0, one launch (start us, length us, event | category | flops | bytes accessed | tf_op | source)
XLA Modules:
  0.0 86.1 jit_solution(9606427613301117022)
XLA Ops:
  7.3 0.8 broadcast_select_fusion
  11.7 0.6 fusion.10
  12.9 0.6 fusion.27
  13.5 0.6 fusion.5
  15.2 19.0 %all-gather.2.cloned.1.call-done = bf16[4,2,16,8192]{3,2,1,0:T(8,128)(2,1)} async-done(((bf16[1,2,16,8192]{3,2,1,0:T(8,128)(2,1)}), bf16[4,2,16,8192]{3,2,1,0:T(8,128)(2,1)}) %all-gather.2.cloned.1.call-update) | async-done | bytes 2097168 | tf_op jit(solution)/shard_map/all_gather | solution.py:112
  34.2 2.0 %reduce_sum.21 = bf16[2,16,8192]{2,1,0:T(8,128)(2,1)S(1)} reduce(bf16[4,2,16,8192]{3,2,1,0:T(8,128)(2,1)} %all-gather.2.cloned.1.call-done, bf16[]{:T(256)} %constant.132.clone.1), dimensions={0}, to_apply=%region_0.1 | reduce | flops 786432 | bytes 2621442 | tf_op jit(solution)/shard_map/reduce_sum | solution.py:112
  39.6 1.4 %fusion.33 = f32[128,16,64]{0,2,1:T(8,128)} fusion(f32[16,64,128]{2,1,0:T(8,128)S(1)} %fusion.16, f32[16,64,128]{2,1,0:T(8,128)S(1)} %fusion.14, f32[64,128]{1,0:T(8,128)S(1)} %get-tuple-element.19, f32[64,128]{1,0:T(8,128)S(1)} %get-tuple-element.20), kind=kOutput, calls=%fused_computation.79 | convolution fusion | flops 101285888 | bytes 1638400 | tf_op jit(solution)/shard_map/rkb,bm->rmk/dot_general | solution.py:56
  41.0 1.6 %negate_bitcast_fusion = (f32[16,128,64]{1,2,0:T(8,128)}, f32[16,128,64]{1,2,0:T(8,128)}) fusion(f32[128,16,64]{0,2,1:T(8,128)S(1)} %fusion.32, f32[16,64,128]{2,1,0:T(8,128)S(1)} %fusion.16, f32[16,64,128]{2,1,0:T(8,128)S(1)} %fusion.14, f32[64,128]{1,0:T(8,128)S(1)} %get-tuple-element.19, f32[64,128]{1,0:T(8,128)S(1)} %get-tuple-element.20), kind=kOutput, calls=%fused_computation.62 | convolution fusion | flops 101810176 | bytes 2686976 | tf_op jit(solution)/shard_map/rkb,bm->rmk/dot_general | solution.py:59
  42.6 1.4 %copy.77 = f32[16,128,64]{2,1,0:T(8,128)S(1)} copy(f32[16,128,64]{1,2,0:T(8,128)} %get-tuple-element.8) | data formatting | bytes 1048576 | tf_op jit(solution)/shard_map/mul | solution.py:90
  44.0 1.0 %mul.962 = f32[16,64,128]{2,1,0:T(8,128)} reshape(f32[16,128,64]{2,1,0:T(8,128)S(1)} %copy.77) | data formatting | bytes 1048576 | tf_op jit(solution)/shard_map/mul | solution.py:90
  45.0 1.4 %copy.79 = f32[16,128,64]{2,1,0:T(8,128)S(1)} copy(f32[16,128,64]{1,2,0:T(8,128)} %get-tuple-element.7) | data formatting | bytes 1048576 | tf_op jit(solution)/shard_map/neg | solution.py:91
  46.4 1.0 %neg.13 = f32[16,64,128]{2,1,0:T(8,128)} reshape(f32[16,128,64]{2,1,0:T(8,128)S(1)} %copy.79) | data formatting | bytes 1048576 | tf_op jit(solution)/shard_map/neg | solution.py:91
  47.4 2.5 %fusion.8 = f32[16,128,64]{1,2,0:T(8,128)} fusion(f32[128,16,64]{0,2,1:T(8,128)} %fusion.33, f32[16,64,128]{2,1,0:T(8,128)S(1)} %fusion.16, f32[16,64,128]{2,1,0:T(8,128)S(1)} %fusion.14, f32[64,128]{1,0:T(8,128)S(1)} %get-tuple-element.19, f32[64,128]{1,0:T(8,128)S(1)} %get-tuple-element.20), kind=kOutput, calls=%fused_computation.25 | convolution fusion | flops 101564416 | bytes 2162688 | tf_op jit(solution)/shard_map/rkb,bm->rmk/dot_general | solution.py:56
  49.9 1.5 %copy.76 = f32[16,128,64]{2,1,0:T(8,128)S(1)} copy(f32[16,128,64]{1,2,0:T(8,128)} %fusion.8) | data formatting | bytes 1048576 | tf_op jit(solution)/shard_map/mul | solution.py:62
  51.3 1.0 %mul.957 = f32[16,64,128]{2,1,0:T(8,128)} reshape(f32[16,128,64]{2,1,0:T(8,128)S(1)} %copy.76) | data formatting | bytes 1048576 | tf_op jit(solution)/shard_map/mul | solution.py:62
  52.3 1.4 %multiply_convert_fusion = (bf16[16,64,128]{2,1,0:T(8,128)(2,1)S(1)}, bf16[16,64,128]{2,1,0:T(8,128)(2,1)S(1)}) fusion(f32[16,64,128]{2,1,0:T(8,128)S(1)} %copy-done.3, f32[16,64,128]{2,1,0:T(8,128)S(1)} %copy-done.2, f32[16,64,128]{2,1,0:T(8,128)} %mul.957), kind=kLoop, calls=%fused_computation.61 | loop fusion | flops 917504 | bytes 2097152 | tf_op jit(solution)/shard_map/convert_element_type | solution.py:91
  57.2 0.6 fusion.20
  58.7 0.6 fusion.19
  60.4 0.7 copy.82
  61.1 1.3 %reshape.211 = bf16[8,2,2560]{2,1,0:T(2,128)(2,1)} reshape(bf16[1280,2,16]{2,1,0:T(2,128)(2,1)S(1)} %bitcast.207) | data formatting | bytes 163840
  62.4 5.5 %all-to-all-start = ((bf16[8,2,2560]{2,1,0:T(2,128)(2,1)}), bf16[8,2,2560]{2,1,0:T(2,128)(2,1)S(1)}, u32[]{:S(2)}, u32[]{:S(2)}) async-start(bf16[8,2,2560]{2,1,0:T(2,128)(2,1)} %reshape.211), calls=%async_computation | async-start | bytes 163840 | tf_op jit(solution)/shard_map/all_to_all | solution.py:134
  68.3 6.7 %all-to-all-done = bf16[8,2,2560]{2,1,0:T(2,128)(2,1)S(1)} async-done(((bf16[8,2,2560]{2,1,0:T(2,128)(2,1)}), bf16[8,2,2560]{2,1,0:T(2,128)(2,1)S(1)}, u32[]{:S(2)}, u32[]{:S(2)}) %all-to-all-start) | async-done | bytes 81952 | tf_op jit(solution)/shard_map/all_to_all | solution.py:134
  75.4 0.6 copy.96
  78.6 0.7 maximum_bitcast_fusion
  (84 shorter events, 16.8 us)
Async XLA Ops:
  6.5 8.4 %copy-start = (f32[64,16]{0,1:T(8,128)S(1)}, f32[64,16]{0,1:T(8,128)}, u32[]{:S(2)}) copy-start(f32[64,16]{0,1:T(8,128)} %param.6) | copy-start | bytes 12292
  6.5 1.6 %copy-start.1 = (bf16[1,2,16,8192]{3,2,1,0:T(8,128)(2,1)S(1)}, bf16[1,2,16,8192]{3,2,1,0:T(8,128)(2,1)}, u32[]{:S(2)}) copy-start(bf16[1,2,16,8192]{3,2,1,0:T(8,128)(2,1)} %param.5) | copy-start | bytes 1572868
  6.5 27.7 %all-gather.2.cloned.1.call-start = ((), (), s32[]{:S(2)}) async-start(), calls=%async_computation.1 | async-start | bytes 2621440 | tf_op jit(solution)/shard_map/all_gather | solution.py:112
  14.1 0.8 copy-start.4
  14.1 0.8 copy-start.5
  49.9 2.5 %copy-start.2 = (f32[16,64,128]{2,1,0:T(8,128)S(1)}, f32[16,64,128]{2,1,0:T(8,128)}, u32[]{:S(2)}) copy-start(f32[16,64,128]{2,1,0:T(8,128)} %mul.962) | copy-start | bytes 1572868
  49.9 2.5 %copy-start.3 = (f32[16,64,128]{2,1,0:T(8,128)S(1)}, f32[16,64,128]{2,1,0:T(8,128)}, u32[]{:S(2)}) copy-start(f32[16,64,128]{2,1,0:T(8,128)} %neg.13) | copy-start | bytes 1572868
  62.4 12.5 %all-to-all-start = ((bf16[8,2,2560]{2,1,0:T(2,128)(2,1)}), bf16[8,2,2560]{2,1,0:T(2,128)(2,1)S(1)}, u32[]{:S(2)}, u32[]{:S(2)}) async-start(bf16[8,2,2560]{2,1,0:T(2,128)(2,1)} %reshape.211), calls=%async_computation | async-start | bytes 163840 | tf_op jit(solution)/shard_map/all_to_all | solution.py:134
Sparse Core Ops, SparseCore 0:
  8.9 25.2 all-gather.1
